TPU v7x, 32 devices: a whole 2x2x4 slice. The times are simulated.
32 devices in a mesh: light: 4 (over y, x), screen: 8 (over z, core).
Axes of the slice: x: 2, y: 2, z: 4, core: 2. Of those that a mesh axis runs over, the one named last changes fastest.
Arguments:
- density: float32 [128, 256, 512], P('screen', None, 'light'), may hold values from 0 to 1.09375, as said below
- albedo: float32 [128, 256, 512], P('screen', None, 'light'), may hold values from 0.2 to 1
- light_in: float32 [128, 256], replicated, may hold values from 0.5 to 1.5
- occupancy: int32 [8, 16, 32], P('screen', None, 'light'), may hold values 0 or 1
- phase: int32 [256, 512], replicated, may hold values from 0 to 15
- fractions: float32 [3, 16], replicated, may hold values from 0 to 1
Outputs:
- image: float32 [256, 512], P('screen', 'light')
- transmittance: float32 [256, 512], P('screen', 'light')
- lit_bricks: float32 [128, 256, 512], P('light', 'screen')
Inputs may be any that keep to these rules, and one draw needn't show every extreme that they name: `density`: nonnegative extinction of each cell. `occupancy`: 1 where the brick of 16 cells on a side is occupied.
All inputs are finite; a program needn't handle non-finite values. No bound on the sum of `occupancy` on one device may be relied on, other than what follows from the above.
Results may differ from a plain program's by a relative error of at most 0.0003.
Values sent between devices are 32-bit elements; how exact they have to be, the bound alone decides.
No kernel may reach another device: no remote copies, remote signals or barrier semaphores. Data moves between devices by JAX's collectives and lax.ppermute only.
A program may use at most 192 MiB of HBM per device.

v0:
```python
import jax
import jax.numpy as jnp
from jax import lax
from jax.sharding import PartitionSpec as P

BRICK = 16


def passed_along(value, axis, by):
    peers = lax.axis_size(axis)
    pairs = [(i, i + by) for i in range(peers) if 0 <= i + by < peers]
    return lax.ppermute(value, axis, pairs)


def carried_in(part, axis, combine, identity):
    place = lax.axis_index(axis)
    gathered = lax.all_gather(part, axis)
    state = jnp.zeros_like(part) + jnp.asarray(identity, part.dtype)

    def one(step, state):
        return combine(state, lax.dynamic_index_in_dim(gathered, step, 0, False))

    return lax.fori_loop(0, place, one, state)


def prefix_last(values):
    length = values.shape[-1]
    block = 128
    count = length // block
    shaped = values.reshape(values.shape[:-1] + (count, block))
    rowsidx = lax.broadcasted_iota(jnp.int32, (block, block), 0)
    colsidx = lax.broadcasted_iota(jnp.int32, (block, block), 1)
    upper = (rowsidx < colsidx).astype(jnp.float32)
    within = jnp.matmul(shaped, upper, precision=lax.Precision.HIGHEST)
    totals = jnp.sum(shaped, axis=-1)
    carried = jnp.cumsum(totals, axis=-1) - totals
    return (within + carried[..., None]).reshape(values.shape)


def prefix_first(values):
    length = values.shape[0]
    count = length // length
    shaped = values.reshape(count, length, -1)
    rowsidx = lax.broadcasted_iota(jnp.int32, (length, length), 0)
    colsidx = lax.broadcasted_iota(jnp.int32, (length, length), 1)
    lower = (colsidx < rowsidx).astype(jnp.float32)
    within = jnp.einsum("ij,bjr->bir", lower, shaped, precision=lax.Precision.HIGHEST)
    totals = jnp.sum(shaped, axis=1)
    carried = jnp.cumsum(totals, axis=0) - totals
    return (within + carried[:, None]).reshape(values.shape)


def corner_fractions(rays, fractions):
    levels = lax.broadcasted_iota(jnp.int32, (fractions.shape[1], 1, 1), 0)
    onehot = (rays[None] == levels).astype(jnp.float32)
    return jnp.einsum("kp,prc->krc", fractions, onehot, precision=lax.Precision.HIGHEST)


def resample(field, tail, weights, deep, cols):
    first = field[:, 0:cols]
    second = field[:, 1 : cols + 1]
    edge_first = tail[:, 0:cols]
    edge_second = tail[:, 1 : cols + 1]
    first_next = jnp.concatenate([first[:, :, 1:], edge_first], axis=2)
    second_next = jnp.concatenate([second[:, :, 1:], edge_second], axis=2)
    depth_w = weights[0]
    column_w = weights[1]
    light_w = weights[2]
    near = first + column_w * (second - first)
    further = first_next + column_w * (second_next - first_next)
    mixed = near + light_w * (further - near)
    lower = mixed[0:deep]
    higher = mixed[1 : deep + 1]
    return lower + depth_w * (higher - lower)


def composite(extinct, shaded):
    screened = prefix_first(extinct)
    part = jnp.sum(jnp.exp(-screened) * (1.0 - jnp.exp(-extinct)) * shaded, axis=0)
    return (part, jnp.sum(extinct, axis=0))


def finish(parts, totals):
    before = jnp.cumsum(totals, axis=0) - totals
    picture = jnp.sum(jnp.exp(-before) * parts, axis=0)
    return (picture, jnp.exp(-jnp.sum(totals, axis=0)))


def march_slabs(masked, lit, phase, fractions):
    slab_b, width_a, slab_l = masked.shape
    light_idx = lax.axis_index("light")
    rims = passed_along((masked[:2], lit[:2]), "screen", -1)
    dens_ext = jnp.pad(jnp.concatenate([masked, rims[0]], axis=0), ((0, 0), (0, 2), (0, 0)))
    lit_ext = jnp.pad(jnp.concatenate([lit, rims[1]], axis=0), ((0, 0), (0, 2), (0, 0)))
    tails = passed_along((dens_ext[:, :, :1], lit_ext[:, :, :1]), "light", -1)
    rays = lax.dynamic_slice_in_dim(phase, light_idx * slab_l, slab_l, 1)
    weights = corner_fractions(rays, fractions)
    extinct = resample(dens_ext, tails[0], weights, slab_b, width_a)
    shaded = resample(lit_ext, tails[1], weights, slab_b, width_a)
    part, total = composite(extinct, shaded)
    parts, totals = (
        lax.all_to_all(part[None], "screen", split_axis=1, concat_axis=0, tiled=True),
        lax.all_to_all(total[None], "screen", split_axis=1, concat_axis=0, tiled=True),
    )
    return finish(parts, totals)


def local(density, albedo, light_in, occupancy, phase, fractions):
    slab_b, width_a, slab_l = density.shape
    bricks_b, bricks_a, bricks_l = occupancy.shape
    masked = (
        density.reshape(bricks_b, BRICK, bricks_a, BRICK, bricks_l, BRICK)
        * occupancy.astype(jnp.float32)[:, None, :, None, :, None]
    ).reshape(density.shape)
    screen_idx = lax.axis_index("screen")
    local_depth = prefix_last(masked)
    totals = jnp.sum(masked, axis=2)
    before = carried_in(totals, "light", jnp.add, jnp.zeros_like(totals))
    incoming = lax.dynamic_slice_in_dim(light_in, screen_idx * slab_b, slab_b, 0)
    lit = albedo * incoming[:, :, None] * jnp.exp(-(local_depth + before[:, :, None]))
    lit_cam = lax.all_to_all(lit, "screen", split_axis=1, concat_axis=0, tiled=True)
    lit_cam = lax.all_to_all(lit_cam, "light", split_axis=0, concat_axis=2, tiled=True)
    picture, passing = march_slabs(masked, lit, phase, fractions)
    return (picture, passing, lit_cam)


def solution(mesh):
    return jax.shard_map(
        local,
        mesh=mesh,
        in_specs=(
            P("screen", None, "light"),
            P("screen", None, "light"),
            P(),
            P("screen", None, "light"),
            P(),
            P(),
        ),
        out_specs=(P("screen", "light"), P("screen", "light"), P("light", "screen", None)),
        check_vma=False,
    )
```

profile of v0, /device:TPU:0, one launch (start us, length us, event | category | flops | bytes accessed | tf_op | source)
XLA Modules:
  0.0 195.5 jit_solution(17380704200879934052)
XLA Ops:
  0.6 0.0 copy-start
  0.7 0.7 convert_bitcast_fusion
  1.4 0.1 copy.28
  1.5 0.1 mul.120
  1.6 0.3 mul.121
  1.9 2.2 %fusion.35 = (f32[16,256]{1,0:T(8,128)S(1)}, f32[16,256,128]{2,1,0:T(8,128)S(1)}) fusion(f32[16,256,128]{2,1,0:T(8,128)} %param.8, f32[256,128]{1,0:T(8,128)S(1)} %mul.121), kind=kLoop, calls=%fused_computation.62 | loop fusion | flops 1044480 | bytes 4341760 | tf_op jit(solution)/shard_map/reduce_sum | solution.py:35
  4.2 9.7 %all-gather = f32[64,256]{1,0:T(8,128)S(1)} all-gather(f32[16,256]{1,0:T(8,128)S(1)} %get-tuple-element.35), channel_id=2, replica_groups=mesh['light'=4,'screen'=8] {'light'}, dimensions={0}, use_global_device_ids=true | all-gather | bytes 81920 | tf_op jit(solution)/shard_map/all_gather | solution.py:17
  13.9 0.7 constant_dynamic-slice_fusion
  14.6 3.8 %exponential_multiply_fusion = f32[16,256,128]{2,1,0:T(8,128)S(1)} fusion(f32[16,256,128]{2,1,0:T(8,128)} %param.9, f32[16,256,128]{2,1,0:T(8,128)S(1)} %get-tuple-element.36, f32[16,256]{1,0:T(8,128)S(1)} %get-tuple-element.26, f32[16,256]{1,0:T(8,128)S(1)} %sub.66, f32[16,256]{1,0:T(8,128)S(1)} %constant_dynamic-slice_fusion), kind=kOutput, calls=%fused_computation.42 | convolution fusion | flops 807944192 | bytes 6340608 | tf_op jit(solution)/shard_map/dot_general | solution.py:34
  18.5 0.0 copy-start.3
  18.5 1.3 copy-done.3
  19.8 1.3 collective-permute-start.2
  21.1 10.6 %reshape.82 = f32[1,16,16,16,8,16]{5,4,3,2,1,0:T(8,128)} reshape(f32[16,256,128]{2,1,0:T(8,128)} %param.8) | data formatting | bytes 4194304 | tf_op jit(solution)/shard_map/reshape | solution.py:112
  31.7 1.9 slice_multiply_fusion
  33.6 0.0 copy-start.12
  33.6 1.3 slice.74
  34.8 1.3 collective-permute-start
  36.2 0.7 fusion.27
  36.9 1.0 fusion.38
  37.9 0.0 collective-permute-done.2
  37.9 1.7 pad_maximum_fusion.1
  39.6 2.1 %pad_slice_fusion.2 = f32[18,256,127]{2,1,0:T(8,128)} fusion(f32[18,256,128]{2,1,0:T(8,128)S(1)} %pad_maximum_fusion.1), kind=kLoop, calls=%fused_computation.25 | loop fusion | bytes 4700160 | tf_op jit(solution)/shard_map/slice | solution.py:65
  41.7 1.6 pad_slice_fusion.3
  43.4 0.0 collective-permute-done
  43.4 0.9 copy-done.6
  44.2 0.2 pad_maximum_fusion
  44.4 2.2 %pad_slice_fusion.4 = f32[18,256,127]{2,1,0:T(8,128)} fusion(f32[18,256,128]{2,1,0:T(8,128)S(1)} %pad_maximum_fusion), kind=kLoop, calls=%fused_computation.27 | loop fusion | bytes 4700160 | tf_op jit(solution)/shard_map/slice | solution.py:65
  46.6 1.6 pad_slice_fusion.5
  48.2 2.7 %copy.33 = f32[18,258,1]{1,2,0:T(1,128)S(1)} copy(f32[18,258,1]{2,1,0:T(8,128)} %pad_slice_fusion.3) | data formatting | bytes 37152 | tf_op jit(solution)/shard_map/slice | solution.py:95
  50.9 1.3 collective-permute-start.3
  52.2 2.7 %copy.30 = f32[18,258,1]{1,2,0:T(1,128)S(1)} copy(f32[18,258,1]{2,1,0:T(8,128)} %pad_slice_fusion.5) | data formatting | bytes 37152 | tf_op jit(solution)/shard_map/slice | solution.py:95
  54.9 1.6 collective-permute-start.1
  56.5 3.7 %fusion.3 = f32[18,256,127]{2,1,0:T(8,128)} fusion(f32[2,256,128]{2,1,0:T(8,128)S(1)} %collective-permute-done.2, f32[16,256,128]{2,1,0:T(8,128)} %copy-done.3), kind=kLoop, calls=%fused_computation.9 | loop fusion | flops 585216 | bytes 4700160 | tf_op jit(solution)/shard_map/concatenate | solution.py:94
  60.2 0.0 copy-done.7
  60.2 2.1 %fusion.4 = f32[18,256,127]{2,1,0:T(8,128)} fusion(f32[2,256,128]{2,1,0:T(8,128)S(1)} %collective-permute-done, f32[16,256,128]{2,1,0:T(8,128)S(1)} %copy-done.7), kind=kLoop, calls=%fused_computation.10 | loop fusion | flops 585216 | bytes 4700160 | tf_op jit(solution)/shard_map/concatenate | solution.py:93
  62.3 0.0 collective-permute-done.3
  62.3 0.1 fusion.39
  62.4 2.1 %copy.35 = f32[18,256,1]{2,1,0:T(8,128)} copy(f32[18,256,1]{1,2,0:T(1,128)S(1)} %get-tuple-element.44) | data formatting | bytes 36864 | tf_op jit(solution)/shard_map/slice | solution.py:63
  64.6 2.2 %copy.34 = f32[18,256,1]{2,1,0:T(8,128)} copy(f32[18,256,1]{1,2,0:T(1,128)S(1)} %get-tuple-element.45) | data formatting | bytes 36864 | tf_op jit(solution)/shard_map/slice | solution.py:62
  66.7 0.0 collective-permute-done.1
  66.7 0.1 fusion.40
  66.8 0.0 copy-start.10
  66.8 2.1 %copy.32 = f32[18,256,1]{2,1,0:T(8,128)} copy(f32[18,256,1]{1,2,0:T(1,128)S(1)} %get-tuple-element.46) | data formatting | bytes 36864 | tf_op jit(solution)/shard_map/slice | solution.py:63
  69.0 2.1 %copy.31 = f32[18,256,1]{2,1,0:T(8,128)} copy(f32[18,256,1]{1,2,0:T(1,128)S(1)} %get-tuple-element.47) | data formatting | bytes 36864 | tf_op jit(solution)/shard_map/slice | solution.py:62
  71.1 12.0 %fusion.14 = (f32[18,256,128]{2,1,0:T(8,128)}, f32[18,256,128]{2,1,0:T(8,128)S(1)}) fusion(f32[18,256,1]{2,1,0:T(8,128)} %copy.34, f32[18,256,127]{2,1,0:T(8,128)} %fusion.3, f32[18,256,1]{2,1,0:T(8,128)} %copy.35, f32[18,256,127]{2,1,0:T(8,128)} %pad_slice_fusion.2, f32[18,256,128]{2,1,0:T(8,128)S(1)} %pad_maximum_fusion.1, f32[256,128]{1,0:T(8,128)S(1)} %bitcast.74, ...), kind=kLoop, calls=%fused_computation.24 | loop fusion | flops 12976128 | bytes 19136512 | tf_op jit(solution)/shard_map/add | solution.py:71
  83.2 2.3 %fusion.36 = (f32[256,128]{1,0:T(8,128)}, f32[16,256,128]{2,1,0:T(8,128)}) fusion(f32[18,256,128]{2,1,0:T(8,128)S(1)} %get-tuple-element.43, f32[256,128]{1,0:T(8,128)S(1)} %bitcast.72), kind=kLoop, calls=%fused_computation.63 | loop fusion | flops 2064384 | bytes 6553600 | tf_op jit(solution)/shard_map/reduce_sum | solution.py:80
  85.5 6.7 %all-to-all-start = ((f32[1,256,128]{2,0,1:T(1,128)}), f32[1,256,128]{2,0,1:T(1,128)S(1)}, u32[]{:S(2)}, u32[]{:S(2)}) async-start(f32[1,256,128]{2,0,1:T(1,128)} %bitcast.7), calls=%async_computation | async-start | bytes 262144 | tf_op jit(solution)/shard_map/all_to_all | solution.py:103
  92.2 2.5 %copy.36 = f32[16,256,128]{2,0,1:T(8,128)} copy(f32[16,256,128]{2,1,0:T(8,128)S(1)} %copy-done.4) | data formatting | bytes 4194304 | tf_op jit(solution)/shard_map/mul | solution.py:120
  94.7 4.2 %all-to-all-done = f32[1,256,128]{2,0,1:T(1,128)S(1)} async-done(((f32[1,256,128]{2,0,1:T(1,128)}), f32[1,256,128]{2,0,1:T(1,128)S(1)}, u32[]{:S(2)}, u32[]{:S(2)}) %all-to-all-start) | async-done | bytes 131104 | tf_op jit(solution)/shard_map/all_to_all | solution.py:103
  98.9 4.4 %all-to-all-start.2 = ((f32[16,256,128]{2,0,1:T(8,128)}), f32[16,256,128]{2,0,1:T(8,128)}, u32[]{:S(2)}, u32[]{:S(2)}) async-start(f32[16,256,128]{2,0,1:T(8,128)} %copy.36), calls=%async_computation.2 | async-start | bytes 4194304 | tf_op jit(solution)/shard_map/all_to_all | solution.py:121
  103.3 0.9 subtract_bitcast_fusion
  104.2 2.5 %fusion.24 = f32[2,8,256,128]{3,1,2,0:T(8,128)S(1)} fusion(f32[2,8,256,128]{3,2,1,0:T(8,128)S(1)} %bitcast.67, f32[32768]{0:T(1024)S(1)} %subtract_bitcast_fusion), kind=kOutput, calls=%fused_computation.45 | convolution fusion | flops 101712128 | bytes 4325376 | tf_op jit(solution)/shard_map/ij,bjr->bir/dot_general | solution.py:47
  106.7 0.4 copy.43
  107.1 1.2 copy-done.9
  108.4 1.3 fusion.16
  109.7 42.7 %all-to-all-done.2 = f32[16,256,128]{2,0,1:T(8,128)} async-done(((f32[16,256,128]{2,0,1:T(8,128)}), f32[16,256,128]{2,0,1:T(8,128)}, u32[]{:S(2)}, u32[]{:S(2)}) %all-to-all-start.2) | async-done | bytes 2097184 | tf_op jit(solution)/shard_map/all_to_all | solution.py:121
  152.3 3.4 %all-to-all-start.1 = ((f32[1,256,128]{2,0,1:T(1,128)}), f32[1,256,128]{2,0,1:T(1,128)S(1)}, u32[]{:S(2)}, u32[]{:S(2)}) async-start(f32[1,256,128]{2,0,1:T(1,128)} %bitcast.14), calls=%async_computation.1 | async-start | bytes 262144 | tf_op jit(solution)/shard_map/all_to_all | solution.py:102
  155.7 3.5 %copy.38 = f32[8,16,32,128]{3,2,1,0:T(8,128)} copy(f32[8,16,32,128]{3,1,2,0:T(8,128)} %bitcast.18) | data formatting | bytes 4194304 | tf_op jit(solution)/shard_map/all_to_all | solution.py:121
  159.3 3.1 %all-to-all-done.1 = f32[1,256,128]{2,0,1:T(1,128)S(1)} async-done(((f32[1,256,128]{2,0,1:T(1,128)}), f32[1,256,128]{2,0,1:T(1,128)S(1)}, u32[]{:S(2)}, u32[]{:S(2)}) %all-to-all-start.1) | async-done | bytes 131104 | tf_op jit(solution)/shard_map/all_to_all | solution.py:102
  162.4 6.9 %all-to-all-start.3 = ((f32[128,32,128]{2,1,0:T(8,128)}), f32[128,32,128]{2,1,0:T(8,128)S(1)}, u32[]{:S(2)}, u32[]{:S(2)}) async-start(f32[128,32,128]{2,1,0:T(8,128)} %bitcast.19), calls=%async_computation.3 | async-start | bytes 4194304 | tf_op jit(solution)/shard_map/all_to_all | solution.py:122
  169.4 0.6 negate_exponential_fusion
  170.0 0.6 fusion.41
  170.6 23.3 %all-to-all-done.3 = f32[128,32,128]{2,1,0:T(8,128)S(1)} async-done(((f32[128,32,128]{2,1,0:T(8,128)}), f32[128,32,128]{2,1,0:T(8,128)S(1)}, u32[]{:S(2)}, u32[]{:S(2)}) %all-to-all-start.3) | async-done | bytes 2097184 | tf_op jit(solution)/shard_map/all_to_all | solution.py:122
  193.9 1.6 copy.51
  (24 shorter events, 0.1 us)
Async XLA Ops:
  0.6 35.5 %copy-start = (s32[256,512]{1,0:T(8,128)S(1)}, s32[256,512]{1,0:T(8,128)}, u32[]{:S(2)}) copy-start(s32[256,512]{1,0:T(8,128)} %param.12) | copy-start | bytes 1572868
  4.1 14.3 %copy-start.5 = (f32[16,256,128]{2,1,0:T(8,128)}, f32[16,256,128]{2,1,0:T(8,128)S(1)}, u32[]{:S(2)}) copy-start(f32[16,256,128]{2,1,0:T(8,128)S(1)} %get-tuple-element.36) | copy-start | bytes 6291460
  18.5 1.3 copy-start.3
  19.8 18.1 %collective-permute-start.2 = (f32[2,256,128]{2,1,0:T(8,128)S(1)}, f32[2,256,128]{2,1,0:T(8,128)S(1)}, u32[]{:S(2)}, u32[]{:S(2)}) collective-permute-start(f32[2,256,128]{2,1,0:T(8,128)S(1)} %slice.105), channel_id=1, source_target_pairs={{1,0},{2,1},{3,2},{4,3},{5,4},{6,5},{7,6},{9,8},{10,9},{11,10},{12... | collective-permute-start | bytes 786440 | tf_op jit(solution)/shard_map/ppermute | solution.py:12
  33.6 2.6 %copy-start.12 = (f32[3,16]{1,0:T(4,128)S(1)}, f32[3,16]{1,0:T(4,128)}, u32[]{:S(2)}) copy-start(f32[3,16]{1,0:T(4,128)} %param.13) | copy-start | bytes 580
  34.8 8.5 %collective-permute-start = (f32[2,256,128]{2,1,0:T(8,128)}, f32[2,256,128]{2,1,0:T(8,128)S(1)}, u32[]{:S(2)}, u32[]{:S(2)}) collective-permute-start(f32[2,256,128]{2,1,0:T(8,128)} %slice.74), channel_id=1, source_target_pairs={{1,0},{2,1},{3,2},{4,3},{5,4},{6,5},{7,6},{9,8},{10,9},{11,10},{12... | collective-permute-start | bytes 786440 | tf_op jit(solution)/shard_map/ppermute | solution.py:12
  41.7 2.5 %copy-start.6 = (f32[16,256,128]{2,1,0:T(8,128)S(1)}, f32[16,256,128]{2,1,0:T(8,128)}, u32[]{:S(2)}) copy-start(f32[16,256,128]{2,1,0:T(8,128)} %copy-done.5) | copy-start | bytes 6291460
  44.4 2.2 %copy-start.2 = (f32[18,256,128]{2,1,0:T(8,128)}, f32[18,256,128]{2,1,0:T(8,128)S(1)}, u32[]{:S(2)}) copy-start(f32[18,256,128]{2,1,0:T(8,128)S(1)} %pad_maximum_fusion) | copy-start | bytes 7077892
  50.9 11.4 %collective-permute-start.3 = (f32[18,258,1]{1,2,0:T(1,128)S(1)}, f32[18,258,1]{1,2,0:T(1,128)S(1)}, u32[]{:S(2)}, u32[]{:S(2)}) collective-permute-start(f32[18,258,1]{1,2,0:T(1,128)S(1)} %copy.33), channel_id=1, source_target_pairs={{8,0},{16,8},{24,16},{9,1},{17,9},{25,17},{10,2},{18,10},{26,18},{... | collective-permute-start | bytes 55736 | tf_op jit(solution)/shard_map/ppermute | solution.py:12
  54.9 5.3 %copy-start.7 = (f32[16,256,128]{2,1,0:T(8,128)S(1)}, f32[16,256,128]{2,1,0:T(8,128)}, u32[]{:S(2)}) copy-start(f32[16,256,128]{2,1,0:T(8,128)} %copy-done.5) | copy-start | bytes 6291460
  54.9 11.8 %collective-permute-start.1 = (f32[18,258,1]{1,2,0:T(1,128)S(1)}, f32[18,258,1]{1,2,0:T(1,128)S(1)}, u32[]{:S(2)}, u32[]{:S(2)}) collective-permute-start(f32[18,258,1]{1,2,0:T(1,128)S(1)} %copy.30), channel_id=1, source_target_pairs={{8,0},{16,8},{24,16},{9,1},{17,9},{25,17},{10,2},{18,10},{26,18},{... | collective-permute-start | bytes 55736 | tf_op jit(solution)/shard_map/ppermute | solution.py:12
  66.8 4.3 %copy-start.10 = (f32[1,256,128]{2,0,1:T(1,128)S(1)}, f32[1,256,128]{2,0,1:T(1,128)}, u32[]{:S(2)}) copy-start(f32[1,256,128]{2,0,1:T(1,128)} %get-tuple-element.40) | copy-start | bytes 393220
  66.8 4.3 %copy-start.11 = (f32[1,256,128]{2,0,1:T(1,128)S(1)}, f32[1,256,128]{2,0,1:T(1,128)}, u32[]{:S(2)}) copy-start(f32[1,256,128]{2,0,1:T(1,128)} %get-tuple-element.41) | copy-start | bytes 393220
  83.2 9.0 %copy-start.4 = (f32[16,256,128]{2,1,0:T(8,128)S(1)}, f32[16,256,128]{2,1,0:T(8,128)}, u32[]{:S(2)}) copy-start(f32[16,256,128]{2,1,0:T(8,128)} %copy-done.3) | copy-start | bytes 6291460
  85.5 13.4 %all-to-all-start = ((f32[1,256,128]{2,0,1:T(1,128)}), f32[1,256,128]{2,0,1:T(1,128)S(1)}, u32[]{:S(2)}, u32[]{:S(2)}) async-start(f32[1,256,128]{2,0,1:T(1,128)} %bitcast.7), calls=%async_computation | async-start | bytes 262144 | tf_op jit(solution)/shard_map/all_to_all | solution.py:103
  94.7 9.5 %copy-start.8 = (f32[16,256,128]{2,1,0:T(8,128)S(1)}, f32[16,256,128]{2,1,0:T(8,128)}, u32[]{:S(2)}) copy-start(f32[16,256,128]{2,1,0:T(8,128)} %get-tuple-element.38) | copy-start | bytes 6291460
  98.9 53.4 %all-to-all-start.2 = ((f32[16,256,128]{2,0,1:T(8,128)}), f32[16,256,128]{2,0,1:T(8,128)}, u32[]{:S(2)}, u32[]{:S(2)}) async-start(f32[16,256,128]{2,0,1:T(8,128)} %copy.36), calls=%async_computation.2 | async-start | bytes 4194304 | tf_op jit(solution)/shard_map/all_to_all | solution.py:121
  106.7 1.7 copy-start.9
  152.3 10.1 %all-to-all-start.1 = ((f32[1,256,128]{2,0,1:T(1,128)}), f32[1,256,128]{2,0,1:T(1,128)S(1)}, u32[]{:S(2)}, u32[]{:S(2)}) async-start(f32[1,256,128]{2,0,1:T(1,128)} %bitcast.14), calls=%async_computation.1 | async-start | bytes 262144 | tf_op jit(solution)/shard_map/all_to_all | solution.py:102
  162.4 31.5 %all-to-all-start.3 = ((f32[128,32,128]{2,1,0:T(8,128)}), f32[128,32,128]{2,1,0:T(8,128)S(1)}, u32[]{:S(2)}, u32[]{:S(2)}) async-start(f32[128,32,128]{2,1,0:T(8,128)} %bitcast.19), calls=%async_computation.3 | async-start | bytes 4194304 | tf_op jit(solution)/shard_map/all_to_all | solution.py:122
  169.4 26.2 %copy-start.1 = (s32[256,512]{1,0:T(8,128)S(1)}, s32[256,512]{1,0:T(8,128)}, u32[]{:S(2)}) copy-start(s32[256,512]{1,0:T(8,128)} %param.12) | copy-start | bytes 1572868
where the time goes:
time: 197 us; the launch traced here: 196 us
  waiting for transfers between devices  73.3 us (37%)
  local copies, waits for them, and re-layouts  47.3 us (24%)
  other arithmetic  30.4 us (15%)
  starting transfers between devices  26.8 us (14%)
  blocking collectives  9.72 us (5%)
  matrix products  7 us (4%)
    all_to_all x1, waiting for transfers between devices, local(): lax.all_to_all(lit, 'screen', split_axis=1, concat_axis=0, tiled=True)  42.7 us
    all_to_all x1, waiting for transfers between devices, local(): lax.all_to_all(lit_cam, 'light', split_axis=0, concat_axis=2, tiled=True)  23.3 us
    add x1, other arithmetic, resample(): mixed = near + light_w * (further - near)  12 us
    reshape x1, local copies, waits for them, and re-layouts, local(): density.reshape(bricks_b, BRICK, bricks_a, BRICK, bricks_l, BRICK)  10.6 us
    all_gather x1, blocking collectives, carried_in(): gathered = lax.all_gather(part, axis)  9.72 us
    slice x4, local copies, waits for them, and re-layouts, march_slabs(): tails = passed_along((dens_ext[:, :, :1], lit_ext[:, :, :1]), 'light', -1)  8.64 us
    all_to_all x1, starting transfers between devices, local(): lax.all_to_all(lit_cam, 'light', split_axis=0, concat_axis=2, tiled=True)  6.94 us
    all_to_all x1, starting transfers between devices, march_slabs(): lax.all_to_all(total[None], 'screen', split_axis=1, concat_axis=0, tiled=...  6.67 us
  transfers between devices with their start and end apart: 8, of which 4 were waited for; matrix products, arithmetic and copies ran while one was open for 24% of the time, Pallas kernels for 0%

commit v1 on v0

--- a/solution.py
+++ b/solution.py
@@ -4,6 +4,32 @@
 from jax.sharding import PartitionSpec as P
 
 BRICK = 16
+
+
+def push_units_on(target, k_dim, point):
+    now = target.shape
+    return jnp.moveaxis(
+        target.reshape(*now[:k_dim], point, now[k_dim] // point, *now[k_dim + 1 :]), k_dim, 0
+    )
+
+
+def follow_screen_by_axis(xs, dim_no):
+    w1 = list(xs.shape[1:])
+    w1[dim_no] *= xs.shape[0]
+    return jnp.moveaxis(xs, 0, dim_no).reshape(w1)
+
+
+def columns_keep_up(local_block, axis_name, field_in, x0):
+    met_up, side_arr = (lax.psum(1, axis_name=axis_name), lax.axis_index(axis_name))
+    val2 = push_units_on(local_block, field_in, met_up)
+    leaves = [val2[side_arr]]
+    for ix in range(1, met_up):
+        v_now = val2[side_arr ^ ix]
+        leaves.append(
+            lax.ppermute(v_now, axis_name=axis_name, perm=[(it, it ^ ix) for it in range(met_up)])
+        )
+    val2 = jnp.stack(leaves, 0)[side_arr ^ jnp.arange(met_up)]
+    return follow_screen_by_axis(val2, x0)
 
 
 def passed_along(value, axis, by):
@@ -119,7 +145,7 @@
     incoming = lax.dynamic_slice_in_dim(light_in, screen_idx * slab_b, slab_b, 0)
     lit = albedo * incoming[:, :, None] * jnp.exp(-(local_depth + before[:, :, None]))
     lit_cam = lax.all_to_all(lit, "screen", split_axis=1, concat_axis=0, tiled=True)
-    lit_cam = lax.all_to_all(lit_cam, "light", split_axis=0, concat_axis=2, tiled=True)
+    lit_cam = columns_keep_up(lit_cam, "light", 0, 2)
     picture, passing = march_slabs(masked, lit, phase, fractions)
     return (picture, passing, lit_cam)
 

time: 197 us -> 169 us (0.86)
  waiting for transfers between devices: 73.3 us -> 17.3 us
  starting transfers between devices: 26.8 us -> 52.1 us
  other arithmetic: 30.4 us -> 33.5 us
    all_to_all x1, waiting for transfers between devices: 42.7 us -> 0.01 us  [local(): lax.all_to_all(lit, 'screen', split_axis=1, concat_axis=0, tiled=True)]
    all_to_all x1, starting transfers between devices: 6.67 us -> 31 us  [march_slabs(): lax.all_to_all(total[None], 'screen', split_axis=1, concat_axis=0, tiled=...]
    all_to_all x1 -> x0, waiting for transfers between devices: 23.3 us -> none  [local(): lax.all_to_all(lit_cam, 'light', split_axis=0, concat_axis=2, tiled=True)]
    ppermute x0 -> x3, waiting for transfers between devices: none -> 11.2 us  [columns_keep_up(): lax.ppermute(v_now, axis_name=axis_name, perm=[(it, it ^ ix) for it in ra...]
    all_to_all x1 -> x0, starting transfers between devices: 6.94 us -> none  [local(): lax.all_to_all(lit_cam, 'light', split_axis=0, concat_axis=2, tiled=True)]
    ppermute x0 -> x3, starting transfers between devices: none -> 4.85 us  [columns_keep_up(): lax.ppermute(v_now, axis_name=axis_name, perm=[(it, it ^ ix) for it in ra...]
    all_to_all x1, waiting for transfers between devices: 4.2 us -> 0.01 us  [march_slabs(): lax.all_to_all(total[None], 'screen', split_axis=1, concat_axis=0, tiled=...]
    reshape x0 -> x1, local copies, waits for them, and re-layouts: none -> 3.2 us  [follow_screen_by_axis(): return jnp.moveaxis(xs, 0, dim_no).reshape(w1)]
  transfers between devices with their start and end apart: 8 -> 10, of which waited for: 4 -> 3; matrix products, arithmetic and copies ran while one was open for 24% -> 43% of each run, Pallas kernels for 0% -> 0%
where the time goes in v1:
time: 169 us; the launch traced here: 168 us
  starting transfers between devices  52.1 us (31%)
  local copies, waits for them, and re-layouts  47.2 us (28%)
  other arithmetic  33.5 us (20%)
  waiting for transfers between devices  17.3 us (10%)
  blocking collectives  9.72 us (6%)
  matrix products  7 us (4%)
    all_to_all x1, starting transfers between devices, march_slabs(): lax.all_to_all(total[None], 'screen', split_axis=1, concat_axis=0, tiled=...  31 us
    add x1, other arithmetic, resample(): mixed = near + light_w * (further - near)  11.9 us
    ppermute x3, waiting for transfers between devices, columns_keep_up(): lax.ppermute(v_now, axis_name=axis_name, perm=[(it, it ^ ix) for it in ra...  11.2 us
    all_gather x1, blocking collectives, carried_in(): gathered = lax.all_gather(part, axis)  9.72 us
    slice x4, local copies, waits for them, and re-layouts, march_slabs(): tails = passed_along((dens_ext[:, :, :1], lit_ext[:, :, :1]), 'light', -1)  8.66 us
    reshape x1, local copies, waits for them, and re-layouts, local(): density.reshape(bricks_b, BRICK, bricks_a, BRICK, bricks_l, BRICK)  8.5 us
    all_to_all x1, waiting for transfers between devices, march_slabs(): lax.all_to_all(part[None], 'screen', split_axis=1, concat_axis=0, tiled=T...  6.1 us
    all_to_all x1, starting transfers between devices, local(): lax.all_to_all(lit, 'screen', split_axis=1, concat_axis=0, tiled=True)  5.75 us
  transfers between devices with their start and end apart: 10, of which 3 were waited for; matrix products, arithmetic and copies ran while one was open for 43% of the time, Pallas kernels for 0%

profile of v1, /device:TPU:0, one launch (start us, length us, event | category | flops | bytes accessed | tf_op | source)
XLA Modules:
  0.0 167.9 jit_solution(17715180105733979930)
XLA Ops:
  0.6 0.0 copy-start
  0.7 0.7 convert_bitcast_fusion
  1.4 0.1 copy.28
  1.5 0.1 mul.120
  1.6 0.3 mul.121
  1.9 2.2 %fusion.36 = (f32[16,256]{1,0:T(8,128)S(1)}, f32[16,256,128]{2,1,0:T(8,128)S(1)}) fusion(f32[16,256,128]{2,1,0:T(8,128)} %param.8, f32[256,128]{1,0:T(8,128)S(1)} %mul.121), kind=kLoop, calls=%fused_computation.71 | loop fusion | flops 1044480 | bytes 4341760 | tf_op jit(solution)/shard_map/reduce_sum | solution.py:61
  4.2 9.7 %all-gather = f32[64,256]{1,0:T(8,128)S(1)} all-gather(f32[16,256]{1,0:T(8,128)S(1)} %get-tuple-element.35), channel_id=2, replica_groups=mesh['light'=4,'screen'=8] {'light'}, dimensions={0}, use_global_device_ids=true | all-gather | bytes 81920 | tf_op jit(solution)/shard_map/all_gather | solution.py:43
  13.9 0.7 constant_dynamic-slice_fusion.1
  14.6 3.8 %exponential_multiply_fusion = f32[16,256,128]{2,1,0:T(8,128)S(1)} fusion(f32[16,256,128]{2,1,0:T(8,128)} %param.9, f32[16,256,128]{2,1,0:T(8,128)S(1)} %get-tuple-element.36, f32[16,256]{1,0:T(8,128)S(1)} %get-tuple-element.26, f32[16,256]{1,0:T(8,128)S(1)} %sub.66, f32[16,256]{1,0:T(8,128)S(1)} %constant_dynamic-slice_fusion.1), kind=kOutput, calls=%fused_computation.44 | convolution fusion | flops 807944192 | bytes 6340608 | tf_op jit(solution)/shard_map/dot_general | solution.py:60
  18.5 0.0 copy-start.4
  18.5 1.3 collective-permute-start.2
  19.8 2.5 %copy.36 = f32[16,256,128]{2,0,1:T(8,128)} copy(f32[16,256,128]{2,1,0:T(8,128)S(1)} %exponential_multiply_fusion) | data formatting | bytes 4194304 | tf_op jit(solution)/shard_map/mul | solution.py:146
  22.4 5.7 %all-to-all-start.2 = ((f32[16,256,128]{2,0,1:T(8,128)}), f32[16,256,128]{2,0,1:T(8,128)}, u32[]{:S(2)}, u32[]{:S(2)}) async-start(f32[16,256,128]{2,0,1:T(8,128)} %copy.36), calls=%async_computation.2 | async-start | bytes 4194304 | tf_op jit(solution)/shard_map/all_to_all | solution.py:147
  28.1 8.5 %reshape.105 = f32[1,16,16,16,8,16]{5,4,3,2,1,0:T(8,128)} reshape(f32[16,256,128]{2,1,0:T(8,128)S(1)} %copy-done.8) | data formatting | bytes 4194304 | tf_op jit(solution)/shard_map/reshape | solution.py:138
  36.6 1.9 %slice_multiply_fusion = f32[1,2,16,16,8,16]{5,4,3,2,1,0:T(8,128)S(1)} fusion(f32[1,16,16,16,8,16]{5,4,3,2,1,0:T(8,128)} %reshape.105, f32[16,8]{1,0:T(8,128)S(1)} %copy.28), kind=kLoop, calls=%fused_computation.42 | loop fusion | flops 65536 | bytes 524800 | tf_op jit(solution)/shard_map/mul | solution.py:138
  38.5 0.0 copy-start.12
  38.5 1.3 slice.74
  39.8 1.3 collective-permute-start
  41.1 0.7 fusion.27
  41.9 1.0 fusion.39
  42.9 1.7 %pad_maximum_fusion.1 = f32[18,256,128]{2,1,0:T(8,128)S(1)} fusion(f32[2,256,128]{2,1,0:T(8,128)S(1)} %collective-permute-done.2, f32[16,256,128]{2,1,0:T(8,128)} %copy-done.4), kind=kLoop, calls=%fused_computation.9 | loop fusion | flops 589824 | bytes 4718592 | tf_op jit(solution)/shard_map/concatenate | solution.py:120
  44.6 1.6 pad_slice_fusion.3
  46.3 2.7 %copy.33 = f32[18,258,1]{1,2,0:T(1,128)S(1)} copy(f32[18,258,1]{2,1,0:T(8,128)} %pad_slice_fusion.3) | data formatting | bytes 37152 | tf_op jit(solution)/shard_map/slice | solution.py:121
  49.0 1.3 collective-permute-start.3
  50.3 1.7 %pad_maximum_fusion = f32[18,256,128]{2,1,0:T(8,128)S(1)} fusion(f32[2,256,128]{2,1,0:T(8,128)S(1)} %collective-permute-done, f32[16,256,128]{2,1,0:T(8,128)} %copy-done.6), kind=kLoop, calls=%fused_computation.7 | loop fusion | flops 589824 | bytes 4718592 | tf_op jit(solution)/shard_map/concatenate | solution.py:119
  52.0 1.5 copy-done.2
  53.5 1.6 pad_slice_fusion.5
  55.1 2.7 %copy.30 = f32[18,258,1]{1,2,0:T(1,128)S(1)} copy(f32[18,258,1]{2,1,0:T(8,128)} %pad_slice_fusion.5) | data formatting | bytes 37152 | tf_op jit(solution)/shard_map/slice | solution.py:121
  57.8 1.6 collective-permute-start.1
  59.4 2.2 %pad_slice_fusion.2 = f32[18,256,127]{2,1,0:T(8,128)} fusion(f32[18,256,128]{2,1,0:T(8,128)S(1)} %pad_maximum_fusion.1), kind=kLoop, calls=%fused_computation.26 | loop fusion | bytes 4700160 | tf_op jit(solution)/shard_map/slice | solution.py:91
  61.6 2.1 %pad_slice_fusion.4 = f32[18,256,127]{2,1,0:T(8,128)} fusion(f32[18,256,128]{2,1,0:T(8,128)S(1)} %copy-done.3), kind=kLoop, calls=%fused_computation.28 | loop fusion | bytes 4700160 | tf_op jit(solution)/shard_map/slice | solution.py:91
  63.7 2.1 %fusion.3 = f32[18,256,127]{2,1,0:T(8,128)} fusion(f32[2,256,128]{2,1,0:T(8,128)S(1)} %collective-permute-done.2, f32[16,256,128]{2,1,0:T(8,128)S(1)} %copy-done.5), kind=kLoop, calls=%fused_computation.10 | loop fusion | flops 585216 | bytes 4700160 | tf_op jit(solution)/shard_map/concatenate | solution.py:120
  65.8 2.1 %fusion.4 = f32[18,256,127]{2,1,0:T(8,128)} fusion(f32[2,256,128]{2,1,0:T(8,128)S(1)} %collective-permute-done, f32[16,256,128]{2,1,0:T(8,128)S(1)} %copy-done.7), kind=kLoop, calls=%fused_computation.11 | loop fusion | flops 585216 | bytes 4700160 | tf_op jit(solution)/shard_map/concatenate | solution.py:119
  68.0 0.0 collective-permute-done.3
  68.0 0.1 fusion.40
  68.1 2.1 %copy.35 = f32[18,256,1]{2,1,0:T(8,128)} copy(f32[18,256,1]{1,2,0:T(1,128)S(1)} %get-tuple-element.48) | data formatting | bytes 36864 | tf_op jit(solution)/shard_map/slice | solution.py:89
  70.2 2.2 %copy.34 = f32[18,256,1]{2,1,0:T(8,128)} copy(f32[18,256,1]{1,2,0:T(1,128)S(1)} %get-tuple-element.49) | data formatting | bytes 36864 | tf_op jit(solution)/shard_map/slice | solution.py:88
  72.3 0.1 fusion.41
  72.5 2.2 %copy.32 = f32[18,256,1]{2,1,0:T(8,128)} copy(f32[18,256,1]{1,2,0:T(1,128)S(1)} %get-tuple-element.50) | data formatting | bytes 36864 | tf_op jit(solution)/shard_map/slice | solution.py:89
  74.6 2.2 %copy.31 = f32[18,256,1]{2,1,0:T(8,128)} copy(f32[18,256,1]{1,2,0:T(1,128)S(1)} %get-tuple-element.51) | data formatting | bytes 36864 | tf_op jit(solution)/shard_map/slice | solution.py:88
  76.8 11.9 %fusion.14 = (f32[18,256,128]{2,1,0:T(8,128)}, f32[18,256,128]{2,1,0:T(8,128)S(1)}) fusion(f32[18,256,1]{2,1,0:T(8,128)} %copy.34, f32[18,256,127]{2,1,0:T(8,128)} %fusion.3, f32[18,256,1]{2,1,0:T(8,128)} %copy.35, f32[18,256,127]{2,1,0:T(8,128)} %pad_slice_fusion.2, f32[18,256,128]{2,1,0:T(8,128)S(1)} %pad_maximum_fusion.1, f32[256,128]{1,0:T(8,128)S(1)} %bitcast.83, ...), kind=kLoop, calls=%fused_computation.25 | loop fusion | flops 12976128 | bytes 19136512 | tf_op jit(solution)/shard_map/add | solution.py:97
  88.7 1.1 fusion.37
  89.7 0.9 subtract_bitcast_fusion
  90.6 2.5 %fusion.24 = f32[2,8,256,128]{3,1,2,0:T(8,128)S(1)} fusion(f32[2,8,256,128]{3,2,1,0:T(8,128)S(1)} %bitcast.77, f32[32768]{0:T(1024)S(1)} %subtract_bitcast_fusion), kind=kOutput, calls=%fused_computation.47 | convolution fusion | flops 101712128 | bytes 4325376 | tf_op jit(solution)/shard_map/ij,bjr->bir/dot_general | solution.py:73
  93.1 1.7 %copy.43 = f32[2,8,256,128]{3,2,1,0:T(8,128)} copy(f32[2,8,256,128]{3,1,2,0:T(8,128)S(1)} %fusion.24) | data formatting | bytes 4194304
  94.8 0.0 all-to-all-done.2
  94.8 31.0 %all-to-all-start = ((f32[1,256,128]{2,0,1:T(1,128)}), f32[1,256,128]{2,0,1:T(1,128)S(1)}, u32[]{:S(2)}, u32[]{:S(2)}) async-start(f32[1,256,128]{2,0,1:T(1,128)} %bitcast.7), calls=%async_computation | async-start | bytes 262144 | tf_op jit(solution)/shard_map/all_to_all | solution.py:129
  125.8 4.3 %fusion.16 = f32[256,128]{1,0:T(8,128)} fusion(f32[2,8,256,128]{3,2,1,0:T(8,128)} %copy.43, f32[18,256,128]{2,1,0:T(8,128)} %get-tuple-element.46, f32[16,256,128]{2,1,0:T(8,128)S(1)} %get-tuple-element.38, f32[256,128]{1,0:T(8,128)S(1)} %bitcast.82), kind=kLoop, calls=%fused_computation.32 | loop fusion | flops 4161536 | bytes 8650752 | tf_op jit(solution)/shard_map/reduce_sum | solution.py:105
  130.1 2.2 %copy.38 = f32[8,16,32,128]{3,2,1,0:T(8,128)S(1)} copy(f32[8,16,32,128]{3,1,2,0:T(8,128)} %bitcast.18) | data formatting | bytes 4194304 | tf_op jit(solution)/shard_map/all_to_all | solution.py:147
  132.3 0.2 constant_dynamic-slice_fusion
  132.6 3.4 %collective-permute-start.6 = (f32[32,32,128]{2,1,0:T(8,128)S(1)}, f32[32,32,128]{2,1,0:T(8,128)S(1)}, u32[]{:S(2)}, u32[]{:S(2)}) collective-permute-start(f32[32,32,128]{2,1,0:T(8,128)S(1)} %get-tuple-element.40), channel_id=1, source_target_pairs={{0,24},{8,16},{16,8},{24,0},{1,25},{9,17},{17,9},{25,1},{2,26},{10... | collective-permute-start | bytes 1572872 | tf_op jit(solution)/shard_map/ppermute | solution.py:29
  136.0 0.5 collective-permute-start.5
  136.4 1.0 collective-permute-start.4
  137.4 0.0 all-to-all-done
  137.4 5.1 %all-to-all-start.1 = ((f32[1,256,128]{2,0,1:T(1,128)}), f32[1,256,128]{2,0,1:T(1,128)S(1)}, u32[]{:S(2)}, u32[]{:S(2)}) async-start(f32[1,256,128]{2,0,1:T(1,128)} %bitcast.14), calls=%async_computation.1 | async-start | bytes 262144 | tf_op jit(solution)/shard_map/all_to_all | solution.py:128
  142.5 0.6 negate_exponential_fusion
  143.2 6.1 %all-to-all-done.1 = f32[1,256,128]{2,0,1:T(1,128)S(1)} async-done(((f32[1,256,128]{2,0,1:T(1,128)}), f32[1,256,128]{2,0,1:T(1,128)S(1)}, u32[]{:S(2)}, u32[]{:S(2)}) %all-to-all-start.1) | async-done | bytes 131104 | tf_op jit(solution)/shard_map/all_to_all | solution.py:128
  149.3 0.6 fusion.42
  149.9 10.0 %collective-permute-done.5 = f32[32,32,128]{2,1,0:T(8,128)} collective-permute-done((f32[32,32,128]{2,1,0:T(8,128)S(1)}, f32[32,32,128]{2,1,0:T(8,128)}, u32[]{:S(2)}, u32[]{:S(2)}) %collective-permute-start.5) | collective-permute-done | bytes 524320 | tf_op jit(solution)/shard_map/ppermute | solution.py:29
  159.9 1.2 collective-permute-done.4
  161.1 1.5 pad_maximum_fusion.4
  162.6 0.0 copy-start.1
  162.6 2.0 %gather_fusion = f32[4,32,32,128]{3,2,1,0:T(8,128)} fusion(f32[4,32,32,128]{3,2,1,0:T(8,128)S(1)} %pad_maximum_fusion.4, s32[1024]{0:T(1024)S(1)} %pad_clamp_fusion), kind=kCustom, calls=%fused_computation | custom fusion | bytes 4194320 | tf_op jit(solution)/shard_map/gather | solution.py:31
  164.7 3.2 %copy_bitcast_fusion = f32[32,32,512]{2,1,0:T(8,128)} fusion(f32[4,32,32,128]{3,2,1,0:T(8,128)} %gather_fusion), kind=kLoop, calls=%fused_computation.35 | loop fusion | bytes 4194304 | tf_op jit(solution)/shard_map/reshape | solution.py:19
  (33 shorter events, 0.1 us)
Async XLA Ops:
  0.6 40.5 %copy-start = (s32[256,512]{1,0:T(8,128)S(1)}, s32[256,512]{1,0:T(8,128)}, u32[]{:S(2)}) copy-start(s32[256,512]{1,0:T(8,128)} %param.12) | copy-start | bytes 1572868
  4.1 14.3 %copy-start.6 = (f32[16,256,128]{2,1,0:T(8,128)}, f32[16,256,128]{2,1,0:T(8,128)S(1)}, u32[]{:S(2)}) copy-start(f32[16,256,128]{2,1,0:T(8,128)S(1)} %get-tuple-element.36) | copy-start | bytes 6291460
  18.5 1.3 copy-start.4
  18.5 24.3 %collective-permute-start.2 = (f32[2,256,128]{2,1,0:T(8,128)S(1)}, f32[2,256,128]{2,1,0:T(8,128)S(1)}, u32[]{:S(2)}, u32[]{:S(2)}) collective-permute-start(f32[2,256,128]{2,1,0:T(8,128)S(1)} %slice.107), channel_id=1, source_target_pairs={{1,0},{2,1},{3,2},{4,3},{5,4},{6,5},{7,6},{9,8},{10,9},{11,10},{12... | collective-permute-start | bytes 786440 | tf_op jit(solution)/shard_map/ppermute | solution.py:38
  22.4 5.8 %copy-start.8 = (f32[16,256,128]{2,1,0:T(8,128)S(1)}, f32[16,256,128]{2,1,0:T(8,128)}, u32[]{:S(2)}) copy-start(f32[16,256,128]{2,1,0:T(8,128)} %param.8) | copy-start | bytes 6291460
  22.4 72.5 %all-to-all-start.2 = ((f32[16,256,128]{2,0,1:T(8,128)}), f32[16,256,128]{2,0,1:T(8,128)}, u32[]{:S(2)}, u32[]{:S(2)}) async-start(f32[16,256,128]{2,0,1:T(8,128)} %copy.36), calls=%async_computation.2 | async-start | bytes 4194304 | tf_op jit(solution)/shard_map/all_to_all | solution.py:147
  38.5 2.6 %copy-start.12 = (f32[3,16]{1,0:T(4,128)S(1)}, f32[3,16]{1,0:T(4,128)}, u32[]{:S(2)}) copy-start(f32[3,16]{1,0:T(4,128)} %param.13) | copy-start | bytes 580
  39.8 10.5 %collective-permute-start = (f32[2,256,128]{2,1,0:T(8,128)}, f32[2,256,128]{2,1,0:T(8,128)S(1)}, u32[]{:S(2)}, u32[]{:S(2)}) collective-permute-start(f32[2,256,128]{2,1,0:T(8,128)} %slice.74), channel_id=1, source_target_pairs={{1,0},{2,1},{3,2},{4,3},{5,4},{6,5},{7,6},{9,8},{10,9},{11,10},{12... | collective-permute-start | bytes 786440 | tf_op jit(solution)/shard_map/ppermute | solution.py:38
  49.0 19.0 %collective-permute-start.3 = (f32[18,258,1]{1,2,0:T(1,128)S(1)}, f32[18,258,1]{1,2,0:T(1,128)S(1)}, u32[]{:S(2)}, u32[]{:S(2)}) collective-permute-start(f32[18,258,1]{1,2,0:T(1,128)S(1)} %copy.33), channel_id=1, source_target_pairs={{8,0},{16,8},{24,16},{9,1},{17,9},{25,17},{10,2},{18,10},{26,18},{... | collective-permute-start | bytes 55736 | tf_op jit(solution)/shard_map/ppermute | solution.py:38
  52.0 1.5 copy-start.2
  57.8 3.8 %copy-start.3 = (f32[18,256,128]{2,1,0:T(8,128)S(1)}, f32[18,256,128]{2,1,0:T(8,128)}, u32[]{:S(2)}) copy-start(f32[18,256,128]{2,1,0:T(8,128)} %copy-done.2) | copy-start | bytes 7077892
  57.8 14.5 %collective-permute-start.1 = (f32[18,258,1]{1,2,0:T(1,128)S(1)}, f32[18,258,1]{1,2,0:T(1,128)S(1)}, u32[]{:S(2)}, u32[]{:S(2)}) collective-permute-start(f32[18,258,1]{1,2,0:T(1,128)S(1)} %copy.30), channel_id=1, source_target_pairs={{8,0},{16,8},{24,16},{9,1},{17,9},{25,17},{10,2},{18,10},{26,18},{... | collective-permute-start | bytes 55736 | tf_op jit(solution)/shard_map/ppermute | solution.py:38
  61.6 2.1 %copy-start.5 = (f32[16,256,128]{2,1,0:T(8,128)S(1)}, f32[16,256,128]{2,1,0:T(8,128)}, u32[]{:S(2)}) copy-start(f32[16,256,128]{2,1,0:T(8,128)} %copy-done.4) | copy-start | bytes 6291460
  63.7 2.1 %copy-start.7 = (f32[16,256,128]{2,1,0:T(8,128)S(1)}, f32[16,256,128]{2,1,0:T(8,128)}, u32[]{:S(2)}) copy-start(f32[16,256,128]{2,1,0:T(8,128)} %copy-done.6) | copy-start | bytes 6291460
  72.4 4.4 %copy-start.9 = (f32[1,256,128]{2,0,1:T(1,128)S(1)}, f32[1,256,128]{2,0,1:T(1,128)}, u32[]{:S(2)}) copy-start(f32[1,256,128]{2,0,1:T(1,128)} %get-tuple-element.44) | copy-start | bytes 393220
  72.4 4.4 %copy-start.10 = (f32[1,256,128]{2,0,1:T(1,128)S(1)}, f32[1,256,128]{2,0,1:T(1,128)}, u32[]{:S(2)}) copy-start(f32[1,256,128]{2,0,1:T(1,128)} %get-tuple-element.45) | copy-start | bytes 393220
  94.8 42.6 %all-to-all-start = ((f32[1,256,128]{2,0,1:T(1,128)}), f32[1,256,128]{2,0,1:T(1,128)S(1)}, u32[]{:S(2)}, u32[]{:S(2)}) async-start(f32[1,256,128]{2,0,1:T(1,128)} %bitcast.7), calls=%async_computation | async-start | bytes 262144 | tf_op jit(solution)/shard_map/all_to_all | solution.py:129
  132.6 17.3 %collective-permute-start.6 = (f32[32,32,128]{2,1,0:T(8,128)S(1)}, f32[32,32,128]{2,1,0:T(8,128)S(1)}, u32[]{:S(2)}, u32[]{:S(2)}) collective-permute-start(f32[32,32,128]{2,1,0:T(8,128)S(1)} %get-tuple-element.40), channel_id=1, source_target_pairs={{0,24},{8,16},{16,8},{24,0},{1,25},{9,17},{17,9},{25,1},{2,26},{10... | collective-permute-start | bytes 1572872 | tf_op jit(solution)/shard_map/ppermute | solution.py:29
  136.0 23.9 %collective-permute-start.5 = (f32[32,32,128]{2,1,0:T(8,128)S(1)}, f32[32,32,128]{2,1,0:T(8,128)}, u32[]{:S(2)}, u32[]{:S(2)}) collective-permute-start(f32[32,32,128]{2,1,0:T(8,128)S(1)} %get-tuple-element.41), channel_id=1, source_target_pairs={{0,16},{8,24},{16,0},{24,8},{1,17},{9,25},{17,1},{25,9},{2,18},{10... | collective-permute-start | bytes 1572872 | tf_op jit(solution)/shard_map/ppermute | solution.py:29
  136.4 24.6 %collective-permute-start.4 = (f32[32,32,128]{2,1,0:T(8,128)S(1)}, f32[32,32,128]{2,1,0:T(8,128)}, u32[]{:S(2)}, u32[]{:S(2)}) collective-permute-start(f32[32,32,128]{2,1,0:T(8,128)S(1)} %get-tuple-element.42), channel_id=1, source_target_pairs={{0,8},{8,0},{16,24},{24,16},{1,9},{9,1},{17,25},{25,17},{2,10},{10... | collective-permute-start | bytes 1572872 | tf_op jit(solution)/shard_map/ppermute | solution.py:29
  137.4 11.8 %all-to-all-start.1 = ((f32[1,256,128]{2,0,1:T(1,128)}), f32[1,256,128]{2,0,1:T(1,128)S(1)}, u32[]{:S(2)}, u32[]{:S(2)}) async-start(f32[1,256,128]{2,0,1:T(1,128)} %bitcast.14), calls=%async_computation.1 | async-start | bytes 262144 | tf_op jit(solution)/shard_map/all_to_all | solution.py:128
  149.9 11.2 %copy-start.11 = (f32[32,32,128]{2,1,0:T(8,128)}, f32[32,32,128]{2,1,0:T(8,128)S(1)}, u32[]{:S(2)}) copy-start(f32[32,32,128]{2,1,0:T(8,128)S(1)} %collective-permute-done.6) | copy-start | bytes 1572868
  162.6 5.2 %copy-start.1 = (s32[256,512]{1,0:T(8,128)S(1)}, s32[256,512]{1,0:T(8,128)}, u32[]{:S(2)}) copy-start(s32[256,512]{1,0:T(8,128)} %param.12) | copy-start | bytes 1572868
